TPU v7x, 32 devices: a whole 2x2x4 slice. The times are simulated.
32 devices in a mesh: dp: 4 (over y, x), seq: 8 (over z, core).
Axes of the slice: x: 2, y: 2, z: 4, core: 2. Of those that a mesh axis runs over, the one named last changes fastest.
Arguments:
- queries: bfloat16 [4, 1024, 2048], P('dp', 'seq'), may hold values from -6 to 6
- key_vectors: bfloat16 [4, 1024, 2048], P('dp', 'seq'), may hold values from -6 to 6
- values: bfloat16 [4, 1024, 2048], P('dp', 'seq'), may hold values from -6 to 6
- out_grad: bfloat16 [4, 1024, 2048], P('dp', 'seq'), may hold values from -6 to 6
- inputs: bfloat16 [4, 1024, 2048], P('dp', 'seq'), may hold values from -6 to 6
Outputs:
- query_grad: bfloat16 [4, 1024, 2048], P('dp', 'seq')
- key_grad: bfloat16 [4, 1024, 2048], P('dp', 'seq')
- value_grad: bfloat16 [4, 1024, 2048], P('dp', 'seq')
- weight_grad: float32 [2048, 2048], P('dp', 'seq')
All inputs are finite; a program needn't handle non-finite values.
Results may differ from a plain program's by a relative error of at most 0.025.
Values may be sent and summed in bfloat16 or wider, within the bound.
No kernel may reach another device: no remote copies, remote signals or barrier semaphores. Data moves between devices by JAX's collectives and lax.ppermute only.
A program may use at most 128 MiB of HBM per device.

v0:
```python
import jax
import jax.numpy as jnp
from jax import lax
from jax.sharding import PartitionSpec as P

HD = 128


def partner(value, axis, apart):
    return lax.ppermute(value, axis, [(i, i ^ 1 << apart) for i in range(lax.axis_size(axis))])


def body(queries, key_vectors, values, out_grad, inputs):
    seq_count = lax.axis_size("seq")
    groups = seq_count // 2
    parity = lax.axis_index("seq") % 2
    is_even = parity == 0
    tok_rows = queries.shape[1]
    half_rows = tok_rows // 2
    width = queries.shape[2]
    group_width = 2 * width // seq_count
    heads_here = group_width // HD
    model_width = inputs.shape[2]
    own_rows = seq_count * half_rows
    length = 2 * own_rows
    doc_rows = own_rows // 4
    block_rows = min(doc_rows, max(256, length // 16))
    block_count = own_rows // block_rows
    scale = HD ** (-0.5)

    def to_heads(array):
        return (
            array[0]
            .reshape(half_rows, 2, groups, group_width)
            .transpose(0, 2, 1, 3)
            .reshape(half_rows, seq_count, group_width)
        )

    moved = (
        lax.all_to_all(to_heads(queries), "seq", split_axis=1, concat_axis=0, tiled=True),
        lax.all_to_all(to_heads(key_vectors), "seq", split_axis=1, concat_axis=0, tiled=True),
        lax.all_to_all(to_heads(values), "seq", split_axis=1, concat_axis=0, tiled=True),
        lax.all_to_all(to_heads(out_grad), "seq", split_axis=1, concat_axis=0, tiled=True),
    )
    q_rows = moved[0].reshape(own_rows, group_width)
    k_rows = moved[1].reshape(own_rows, group_width)
    v_rows = moved[2].reshape(own_rows, group_width)
    g_rows = moved[3].reshape(own_rows, group_width)
    k_other, v_other = partner((k_rows, v_rows), "seq", 0)

    def in_order(mine, theirs):
        even_rows = jnp.where(is_even, mine, theirs)
        odd_rows = jnp.where(is_even, theirs, mine)
        return jnp.stack([even_rows, odd_rows], axis=1).reshape(2 * mine.shape[0], mine.shape[1])

    key_all = in_order(k_rows, k_other).reshape(length, heads_here, HD)
    value_all = in_order(v_rows, v_other).reshape(length, heads_here, HD)
    query_heads = q_rows.reshape(own_rows, heads_here, HD)
    grad_heads = g_rows.reshape(own_rows, heads_here, HD)
    key_total = jnp.zeros((length, heads_here, HD), jnp.float32)
    value_total = jnp.zeros((length, heads_here, HD), jnp.float32)
    query_parts = []
    for block in range(block_count):
        start = block * block_rows
        stop = start + block_rows
        low = 2 * (start // doc_rows * doc_rows)
        high = 2 * stop
        query_block = query_heads[start:stop]
        grad_block = grad_heads[start:stop]
        key_block = key_all[low:high]
        value_block = value_all[low:high]
        scores = (
            jnp.einsum("qhd,khd->hqk", query_block, key_block, preferred_element_type=jnp.float32)
            * scale
        )
        query_pos = 2 * (start + jnp.arange(block_rows, dtype=jnp.int32)) + parity
        key_pos = low + jnp.arange(high - low, dtype=jnp.int32)
        visible = key_pos[None, :] <= query_pos[:, None]
        scores = jnp.where(visible[None], scores, -jnp.inf)
        top = jnp.max(scores, axis=2, keepdims=True)
        weights = jnp.exp(scores - top)
        probs = weights / jnp.sum(weights, axis=2, keepdims=True)
        probs_low = probs.astype(jnp.bfloat16)
        dprob = jnp.einsum(
            "qhd,khd->hqk", grad_block, value_block, preferred_element_type=jnp.float32
        )
        delta = jnp.sum(probs * dprob, axis=2, keepdims=True)
        dscore = (probs * (dprob - delta) * scale).astype(jnp.bfloat16)
        query_parts.append(
            jnp.einsum(
                "hqk,khd->qhd", dscore, key_block, preferred_element_type=jnp.float32
            ).astype(jnp.bfloat16)
        )
        key_total = key_total.at[low:high].add(
            jnp.einsum("hqk,qhd->khd", dscore, query_block, preferred_element_type=jnp.float32)
        )
        value_total = value_total.at[low:high].add(
            jnp.einsum("hqk,qhd->khd", probs_low, grad_block, preferred_element_type=jnp.float32)
        )
    query_grad = jnp.concatenate(query_parts, axis=0).reshape(own_rows, group_width)

    def by_parity(total):
        paired = total.reshape(own_rows, 2, group_width)
        mine = jnp.where(is_even, paired[:, 0], paired[:, 1])
        theirs = jnp.where(is_even, paired[:, 1], paired[:, 0])
        return (mine.astype(jnp.bfloat16), theirs.astype(jnp.bfloat16))

    key_mine, key_theirs = by_parity(key_total)
    value_mine, value_theirs = by_parity(value_total)
    key_back, value_back = partner((key_theirs, value_theirs), "seq", 0)
    key_grad = (key_mine.astype(jnp.float32) + key_back.astype(jnp.float32)).astype(jnp.bfloat16)
    value_grad = (value_mine.astype(jnp.float32) + value_back.astype(jnp.float32)).astype(
        jnp.bfloat16
    )
    spread = jnp.broadcast_to(
        inputs[0].reshape(half_rows, 1, 2, model_width), (half_rows, groups, 2, model_width)
    ).reshape(half_rows, seq_count, model_width)
    input_rows = lax.all_to_all(spread, "seq", split_axis=1, concat_axis=0, tiled=True).reshape(
        own_rows, model_width
    )
    term = jnp.einsum("td,tc->dc", input_rows, value_grad, preferred_element_type=jnp.float32)
    halves = term.reshape(term.shape[0], 2, term.shape[1] // 2)
    mine = jnp.where(is_even, halves[:, 0], halves[:, 1])
    theirs = jnp.where(is_even, halves[:, 1], halves[:, 0])
    mine, theirs = (mine, theirs)
    received = partner(theirs.astype(jnp.bfloat16), "seq", 0).astype(theirs.dtype)
    weight_grad = lax.psum_scatter(
        (mine + received).astype(jnp.bfloat16), "dp", scatter_dimension=0, tiled=True
    ).astype(jnp.float32)

    def to_tokens(array):
        return array.reshape(seq_count, half_rows, 1, group_width)

    def from_heads(array):
        return (
            array.reshape(half_rows, groups, 2, group_width)
            .transpose(0, 2, 1, 3)
            .reshape(1, tok_rows, width)
        )

    returned = (
        lax.all_to_all(to_tokens(query_grad), "seq", split_axis=0, concat_axis=2, tiled=True),
        lax.all_to_all(to_tokens(key_grad), "seq", split_axis=0, concat_axis=2, tiled=True),
        lax.all_to_all(to_tokens(value_grad), "seq", split_axis=0, concat_axis=2, tiled=True),
    )
    return (from_heads(returned[0]), from_heads(returned[1]), from_heads(returned[2]), weight_grad)


def solution(mesh):
    return jax.shard_map(
        body,
        mesh=mesh,
        in_specs=(
            P("dp", "seq", None),
            P("dp", "seq", None),
            P("dp", "seq", None),
            P("dp", "seq", None),
            P("dp", "seq", None),
        ),
        out_specs=(
            P("dp", "seq", None),
            P("dp", "seq", None),
            P("dp", "seq", None),
            P("dp", "seq"),
        ),
        check_vma=False,
    )
```

profile of v0, /device:TPU:0, one launch (start us, length us, event | category | flops | bytes accessed | tf_op | source)
XLA Modules:
  0.0 255.6 jit_solution(17739342030090548654)
XLA Ops:
  9.6 6.5 %all-to-all-start.2 = ((bf16[64,8,512]{2,0,1:T(8,128)(2,1)}), bf16[64,8,512]{2,0,1:T(8,128)(2,1)S(1)}, u32[]{:S(2)}, u32[]{:S(2)}) async-start(bf16[64,8,512]{2,0,1:T(8,128)(2,1)} %bitcast.15), calls=%async_computation.2 | async-start | bytes 1048576 | tf_op jit(solution)/shard_map/all_to_all | solution.py:42
  17.4 14.0 %all-to-all-done.2 = bf16[64,8,512]{2,0,1:T(8,128)(2,1)S(1)} async-done(((bf16[64,8,512]{2,0,1:T(8,128)(2,1)}), bf16[64,8,512]{2,0,1:T(8,128)(2,1)S(1)}, u32[]{:S(2)}, u32[]{:S(2)}) %all-to-all-start.2) | async-done | bytes 524320 | tf_op jit(solution)/shard_map/all_to_all | solution.py:42
  31.4 3.6 %all-to-all-start.3 = ((bf16[64,8,512]{2,0,1:T(8,128)(2,1)}), bf16[64,8,512]{2,0,1:T(8,128)(2,1)S(1)}, u32[]{:S(2)}, u32[]{:S(2)}) async-start(bf16[64,8,512]{2,0,1:T(8,128)(2,1)} %bitcast.24), calls=%async_computation.3 | async-start | bytes 1048576 | tf_op jit(solution)/shard_map/all_to_all | solution.py:43
  36.4 13.9 %all-to-all-done.3 = bf16[64,8,512]{2,0,1:T(8,128)(2,1)S(1)} async-done(((bf16[64,8,512]{2,0,1:T(8,128)(2,1)}), bf16[64,8,512]{2,0,1:T(8,128)(2,1)S(1)}, u32[]{:S(2)}, u32[]{:S(2)}) %all-to-all-start.3) | async-done | bytes 524320 | tf_op jit(solution)/shard_map/all_to_all | solution.py:43
  50.4 3.5 %all-to-all-start = ((bf16[64,8,512]{2,0,1:T(8,128)(2,1)}), bf16[64,8,512]{2,0,1:T(8,128)(2,1)S(1)}, u32[]{:S(2)}, u32[]{:S(2)}) async-start(bf16[64,8,512]{2,0,1:T(8,128)(2,1)} %bitcast.1), calls=%async_computation | async-start | bytes 1048576 | tf_op jit(solution)/shard_map/all_to_all | solution.py:41
  55.9 13.2 %all-to-all-done = bf16[64,8,512]{2,0,1:T(8,128)(2,1)S(1)} async-done(((bf16[64,8,512]{2,0,1:T(8,128)(2,1)}), bf16[64,8,512]{2,0,1:T(8,128)(2,1)S(1)}, u32[]{:S(2)}, u32[]{:S(2)}) %all-to-all-start) | async-done | bytes 524320 | tf_op jit(solution)/shard_map/all_to_all | solution.py:41
  69.1 3.5 %all-to-all-start.1 = ((bf16[64,8,512]{2,0,1:T(8,128)(2,1)}), bf16[64,8,512]{2,0,1:T(8,128)(2,1)S(1)}, u32[]{:S(2)}, u32[]{:S(2)}) async-start(bf16[64,8,512]{2,0,1:T(8,128)(2,1)} %bitcast.10), calls=%async_computation.1 | async-start | bytes 1048576 | tf_op jit(solution)/shard_map/all_to_all | solution.py:40
  77.6 10.3 %all-to-all-done.1 = bf16[64,8,512]{2,0,1:T(8,128)(2,1)S(1)} async-done(((bf16[64,8,512]{2,0,1:T(8,128)(2,1)}), bf16[64,8,512]{2,0,1:T(8,128)(2,1)S(1)}, u32[]{:S(2)}, u32[]{:S(2)}) %all-to-all-start.1) | async-done | bytes 524320 | tf_op jit(solution)/shard_map/all_to_all | solution.py:40
  87.9 1.6 broadcast_in_dim.67
  89.5 3.8 %all-to-all-start.7 = ((bf16[64,8,2048]{2,0,1:T(8,128)(2,1)}), bf16[64,8,2048]{2,0,1:T(8,128)(2,1)S(1)}, u32[]{:S(2)}, u32[]{:S(2)}) async-start(bf16[64,8,2048]{2,0,1:T(8,128)(2,1)} %bitcast.65), calls=%async_computation.7 | async-start | bytes 4194304 | tf_op jit(solution)/shard_map/all_to_all | solution.py:118
  93.3 1.9 fusion.219
  96.8 1.6 slice.325
  100.7 1.6 slice.313
  110.2 2.1 fusion.236
  112.3 2.3 convolution_bitcast_fusion.3
  114.6 2.5 scatter-add.34
  117.1 2.1 fusion.221
  119.2 2.2 fusion.231
  121.4 2.4 fusion.17
  124.2 1.9 fusion.226
  126.1 2.4 fusion.24
  133.6 2.5 fusion.26
  136.2 3.9 %copy.167 = bf16[1024,4,128]{2,1,0:T(4,128)(2,1)} copy(f32[1024,4,128]{2,0,1:T(8,128)} %fusion.26) | data formatting | bytes 3145728 | tf_op jit(solution)/shard_map/scatter-add | solution.py:97
  141.6 3.0 %fusion.60 = (bf16[512,1,512]{2,1,0:T(2,128)(2,1)S(1)}, f32[512,1,512]{2,1,0:T(1,128)}) fusion(pred[]{:T(512)S(6)} %eq.5, bf16[512,2,512]{2,1,0:T(2,128)(2,1)S(1)} %reshape.498), kind=kLoop, calls=%fused_computation.98 | loop fusion | flops 786432 | bytes 2621441 | tf_op jit(solution)/shard_map/convert_element_type | solution.py:106
  146.0 2.4 fusion.54
  148.5 2.0 convolution_bitcast_fusion.9
  150.4 2.7 %fusion.53 = bf16[128,4,128]{2,0,1:T(8,128)(2,1)} fusion(f32[4,128,256]{1,2,0:T(8,128)} %convolution_bitcast_fusion.9, bf16[256,4,128]{2,1,0:T(4,128)(2,1)} %copy-done.18, f32[4,128,256]{1,2,0:T(8,128)} %get-tuple-element.129, f32[4,128]{1,0:T(4,128)S(1)} %get-tuple-element.128), kind=kOutput, calls=%fused_computation.91 | convolution fusion | flops 34538240 | bytes 1443840 | tf_op jit(solution)/shard_map/hqk,khd->qhd/dot_general | solution.py:90
  154.2 2.7 %fusion.52 = bf16[128,4,128]{2,0,1:T(8,128)(2,1)} fusion(f32[4,128,256]{1,2,0:T(8,128)} %convolution_bitcast_fusion.10, bf16[256,4,128]{2,1,0:T(4,128)(2,1)} %slice.311, f32[4,128,256]{1,2,0:T(8,128)} %get-tuple-element.131, f32[4,128]{1,0:T(4,128)S(1)} %get-tuple-element.130), kind=kOutput, calls=%fused_computation.90 | convolution fusion | flops 34538240 | bytes 1443840 | tf_op jit(solution)/shard_map/hqk,khd->qhd/dot_general | solution.py:90
  157.2 1.6 fusion.51
  160.3 2.4 convolution_bitcast_fusion.7
  162.7 2.6 %scatter-add.26 = f32[1024,4,128]{2,0,1:T(8,128)} pad(f32[256,4,128]{2,0,1:T(8,128)} %convolution_bitcast_fusion.7, f32[]{:T(128)} %constant.216.clone.1), padding=0_768x0_0x0_0 | pad | bytes 2621444 | tf_op jit(solution)/shard_map/scatter-add | solution.py:94
  165.3 2.8 %fusion.18 = f32[1024,4,128]{2,0,1:T(8,128)} fusion(f32[1024,4,128]{2,0,1:T(8,128)} %scatter-add.26, f32[4,128,256]{1,2,0:T(8,128)} %convolution_bitcast_fusion.10, bf16[128,4,128]{2,1,0:T(4,128)(2,1)S(1)} %copy-done.23, f32[4,128,256]{1,2,0:T(8,128)} %get-tuple-element.131, f32[4,128]{1,0:T(4,128)S(1)} %get-tuple-element.130), kind=kOutput, calls=%fused_computation.43 | convolution fusion | flops 34472704 | bytes 2756608 | tf_op jit(solution)/shard_map/hqk,qhd->khd/dot_general | solution.py:95
  168.1 2.1 fusion.62
  170.1 4.8 %all-to-all-start.4 = ((bf16[8,64,1,512]{3,1,2,0:T(8,128)(2,1)}), bf16[8,64,1,512]{3,1,2,0:T(8,128)(2,1)}, u32[]{:S(2)}, u32[]{:S(2)}) async-start(bf16[8,64,1,512]{3,1,2,0:T(8,128)(2,1)} %bitcast.239), calls=%async_computation.4 | async-start | bytes 1048576 | tf_op jit(solution)/shard_map/all_to_all | solution.py:142
  174.9 2.3 fusion.241
  177.3 2.2 fusion.218
  179.5 1.9 copy.182
  181.4 2.9 %copy.181 = f32[2048,1,256]{2,0,1:T(8,128)} copy(f32[2048,1,256]{0,2,1:T(8,128)} %get-tuple-element.100) | data formatting | bytes 4194304
  185.6 2.1 collective-permute-start.4
  187.7 2.8 %fusion.20 = f32[1024,4,128]{2,0,1:T(8,128)} fusion(f32[1024,4,128]{2,0,1:T(8,128)} %fusion.18, f32[4,128,256]{1,2,0:T(8,128)} %convolution_bitcast_fusion.9, bf16[128,4,128]{2,1,0:T(4,128)(2,1)S(1)} %copy-done.22, f32[4,128,256]{1,2,0:T(8,128)} %get-tuple-element.129, f32[4,128]{1,0:T(4,128)S(1)} %get-tuple-element.128), kind=kOutput, calls=%fused_computation.50 | convolution fusion | flops 34603776 | bytes 3280896 | tf_op jit(solution)/shard_map/hqk,qhd->khd/dot_general | solution.py:95
  190.5 2.8 %fusion.22 = f32[1024,4,128]{2,0,1:T(8,128)} fusion(f32[1024,4,128]{2,0,1:T(8,128)} %fusion.20, f32[4,128,256]{1,2,0:T(8,128)} %copy-done.7, bf16[128,4,128]{2,1,0:T(4,128)(2,1)S(1)} %copy-done.20, f32[4,128,256]{1,2,0:T(8,128)} %get-tuple-element.127, f32[4,128]{1,0:T(4,128)S(1)} %get-tuple-element.126), kind=kOutput, calls=%fused_computation.52 | convolution fusion | flops 34603776 | bytes 3280896 | tf_op jit(solution)/shard_map/hqk,qhd->khd/dot_general | solution.py:95
  193.3 3.9 %copy.160 = bf16[1024,4,128]{2,1,0:T(4,128)(2,1)} copy(f32[1024,4,128]{2,0,1:T(8,128)} %fusion.22) | data formatting | bytes 3145728 | tf_op jit(solution)/shard_map/scatter-add | solution.py:94
  198.7 3.0 %fusion.57 = (bf16[512,1,512]{2,1,0:T(2,128)(2,1)S(1)}, f32[512,1,512]{2,1,0:T(1,128)}) fusion(pred[]{:T(512)S(6)} %eq.5, bf16[512,2,512]{2,1,0:T(2,128)(2,1)S(1)} %reshape.494), kind=kLoop, calls=%fused_computation.95 | loop fusion | flops 786432 | bytes 2621441 | tf_op jit(solution)/shard_map/convert_element_type | solution.py:106
  202.7 2.7 %fusion.8 = bf16[2048,256]{1,0:T(8,128)(2,1)} fusion(bf16[2048,256]{1,0:T(8,128)(2,1)} %collective-permute-done.4, f32[2048,1,256]{2,0,1:T(8,128)S(1)} %copy-done, f32[2048,1,256]{2,0,1:T(8,128)S(1)} %copy.182, pred[]{:T(512)S(6)} %eq.5), kind=kLoop, calls=%fused_computation.9 | loop fusion | flops 2097152 | bytes 6291457 | tf_op jit(solution)/shard_map/convert_element_type | solution.py:128
  206.7 19.9 %all_to_all.120 = bf16[8,64,1,512]{3,1,2,0:T(8,128)(2,1)S(1)} all-to-all(bf16[8,64,1,512]{3,1,2,0:T(8,128)(2,1)S(1)} %bitcast.248), channel_id=1, replica_groups=mesh['dp'=4,'seq'=8] {'seq'}, dimensions={0} | all-to-all | bytes 1048576 | tf_op jit(solution)/shard_map/all_to_all | solution.py:143
  226.6 3.8 %all-to-all-start.6 = ((bf16[8,64,1,512]{3,1,2,0:T(8,128)(2,1)}), bf16[8,64,1,512]{3,1,2,0:T(8,128)(2,1)S(1)}, u32[]{:S(2)}, u32[]{:S(2)}) async-start(bf16[8,64,1,512]{3,1,2,0:T(8,128)(2,1)} %bitcast.60), calls=%async_computation.6 | async-start | bytes 1048576 | tf_op jit(solution)/shard_map/all_to_all | solution.py:144
  234.6 10.8 %all-to-all-done.6 = bf16[8,64,1,512]{3,1,2,0:T(8,128)(2,1)S(1)} async-done(((bf16[8,64,1,512]{3,1,2,0:T(8,128)(2,1)}), bf16[8,64,1,512]{3,1,2,0:T(8,128)(2,1)S(1)}, u32[]{:S(2)}, u32[]{:S(2)}) %all-to-all-start.6) | async-done | bytes 524320 | tf_op jit(solution)/shard_map/all_to_all | solution.py:144
  247.0 1.8 convert_element_type.141
  (134 shorter events, 45.7 us)
Async XLA Ops:
  7.2 8.9 %copy-start.12 = (bf16[1,128,2048]{2,1,0:T(8,128)(2,1)S(1)}, bf16[1,128,2048]{2,1,0:T(8,128)(2,1)}, u32[]{:S(2)}) copy-start(bf16[1,128,2048]{2,1,0:T(8,128)(2,1)} %param.24) | copy-start | bytes 1572868
  9.6 25.5 %copy-start.13 = (bf16[1,128,2048]{2,1,0:T(8,128)(2,1)S(1)}, bf16[1,128,2048]{2,1,0:T(8,128)(2,1)}, u32[]{:S(2)}) copy-start(bf16[1,128,2048]{2,1,0:T(8,128)(2,1)} %param.22) | copy-start | bytes 1572868
  9.6 21.8 %all-to-all-start.2 = ((bf16[64,8,512]{2,0,1:T(8,128)(2,1)}), bf16[64,8,512]{2,0,1:T(8,128)(2,1)S(1)}, u32[]{:S(2)}, u32[]{:S(2)}) async-start(bf16[64,8,512]{2,0,1:T(8,128)(2,1)} %bitcast.15), calls=%async_computation.2 | async-start | bytes 1048576 | tf_op jit(solution)/shard_map/all_to_all | solution.py:42
  31.4 22.4 %copy-start.14 = (bf16[1,128,2048]{2,1,0:T(8,128)(2,1)S(1)}, bf16[1,128,2048]{2,1,0:T(8,128)(2,1)}, u32[]{:S(2)}) copy-start(bf16[1,128,2048]{2,1,0:T(8,128)(2,1)} %param.21) | copy-start | bytes 1572868
  31.4 18.9 %all-to-all-start.3 = ((bf16[64,8,512]{2,0,1:T(8,128)(2,1)}), bf16[64,8,512]{2,0,1:T(8,128)(2,1)S(1)}, u32[]{:S(2)}, u32[]{:S(2)}) async-start(bf16[64,8,512]{2,0,1:T(8,128)(2,1)} %bitcast.24), calls=%async_computation.3 | async-start | bytes 1048576 | tf_op jit(solution)/shard_map/all_to_all | solution.py:43
  50.4 18.8 %all-to-all-start = ((bf16[64,8,512]{2,0,1:T(8,128)(2,1)}), bf16[64,8,512]{2,0,1:T(8,128)(2,1)S(1)}, u32[]{:S(2)}, u32[]{:S(2)}) async-start(bf16[64,8,512]{2,0,1:T(8,128)(2,1)} %bitcast.1), calls=%async_computation | async-start | bytes 1048576 | tf_op jit(solution)/shard_map/all_to_all | solution.py:41
  69.1 18.8 %all-to-all-start.1 = ((bf16[64,8,512]{2,0,1:T(8,128)(2,1)}), bf16[64,8,512]{2,0,1:T(8,128)(2,1)S(1)}, u32[]{:S(2)}, u32[]{:S(2)}) async-start(bf16[64,8,512]{2,0,1:T(8,128)(2,1)} %bitcast.10), calls=%async_computation.1 | async-start | bytes 1048576 | tf_op jit(solution)/shard_map/all_to_all | solution.py:40
  74.1 30.5 %collective-permute-start = (bf16[512,512]{1,0:T(8,128)(2,1)S(1)}, bf16[512,512]{1,0:T(8,128)(2,1)}, u32[]{:S(2)}, u32[]{:S(2)}) collective-permute-start(bf16[512,512]{1,0:T(8,128)(2,1)S(1)} %bitcast.238), channel_id=1, source_target_pairs={{0,1},{1,0},{2,3},{3,2},{4,5},{5,4},{6,7},{7,6},{8,9},{9,8},{10,11... | collective-permute-start | bytes 1572872 | tf_op jit(solution)/shard_map/ppermute | solution.py:10
  76.6 51.8 %collective-permute-start.1 = (bf16[512,512]{1,0:T(8,128)(2,1)S(1)}, bf16[512,512]{1,0:T(8,128)(2,1)}, u32[]{:S(2)}, u32[]{:S(2)}) collective-permute-start(bf16[512,512]{1,0:T(8,128)(2,1)S(1)} %bitcast.237), channel_id=1, source_target_pairs={{0,1},{1,0},{2,3},{3,2},{4,5},{5,4},{6,7},{7,6},{8,9},{9,8},{10,11... | collective-permute-start | bytes 1572872 | tf_op jit(solution)/shard_map/ppermute | solution.py:10
  87.9 1.6 copy-start.3
  89.5 80.6 %all-to-all-start.7 = ((bf16[64,8,2048]{2,0,1:T(8,128)(2,1)}), bf16[64,8,2048]{2,0,1:T(8,128)(2,1)S(1)}, u32[]{:S(2)}, u32[]{:S(2)}) async-start(bf16[64,8,2048]{2,0,1:T(8,128)(2,1)} %bitcast.65), calls=%async_computation.7 | async-start | bytes 4194304 | tf_op jit(solution)/shard_map/all_to_all | solution.py:118
  110.1 6.9 %copy-start.15 = (bf16[256,4,128]{2,1,0:T(4,128)(2,1)}, bf16[256,4,128]{2,1,0:T(4,128)(2,1)S(1)}, u32[]{:S(2)}) copy-start(bf16[256,4,128]{2,1,0:T(4,128)(2,1)S(1)} %slice.303) | copy-start | bytes 786436
  112.3 4.8 %copy-start.19 = (bf16[128,4,128]{2,1,0:T(4,128)(2,1)S(1)}, bf16[128,4,128]{2,1,0:T(4,128)(2,1)}, u32[]{:S(2)}) copy-start(bf16[128,4,128]{2,1,0:T(4,128)(2,1)} %slice.329) | copy-start | bytes 393220
  117.1 4.3 %copy-start.9 = (bf16[128,4,128]{2,1,0:T(4,128)(2,1)S(1)}, bf16[128,4,128]{2,1,0:T(4,128)(2,1)}, u32[]{:S(2)}) copy-start(bf16[128,4,128]{2,1,0:T(4,128)(2,1)} %slice.317) | copy-start | bytes 393220
  121.4 2.8 %copy-start.21 = (bf16[128,4,128]{2,1,0:T(4,128)(2,1)S(1)}, bf16[128,4,128]{2,1,0:T(4,128)(2,1)}, u32[]{:S(2)}) copy-start(bf16[128,4,128]{2,1,0:T(4,128)(2,1)} %slice.321) | copy-start | bytes 393220
  121.4 4.7 %copy-start.11 = (bf16[128,4,128]{2,1,0:T(4,128)(2,1)S(1)}, bf16[128,4,128]{2,1,0:T(4,128)(2,1)}, u32[]{:S(2)}) copy-start(bf16[128,4,128]{2,1,0:T(4,128)(2,1)} %slice.325) | copy-start | bytes 393220
  124.2 4.3 %copy-start.18 = (bf16[256,4,128]{2,1,0:T(4,128)(2,1)}, bf16[256,4,128]{2,1,0:T(4,128)(2,1)S(1)}, u32[]{:S(2)}) copy-start(bf16[256,4,128]{2,1,0:T(4,128)(2,1)S(1)} %slice.319) | copy-start | bytes 786436
  141.5 4.2 %copy-start.6 = (bf16[256,4,128]{2,1,0:T(4,128)(2,1)S(1)}, bf16[256,4,128]{2,1,0:T(4,128)(2,1)}, u32[]{:S(2)}) copy-start(bf16[256,4,128]{2,1,0:T(4,128)(2,1)} %slice.331) | copy-start | bytes 786436
  144.6 1.4 copy-start.17
  145.5 2.9 %copy-start.5 = (bf16[256,4,128]{2,1,0:T(4,128)(2,1)S(1)}, bf16[256,4,128]{2,1,0:T(4,128)(2,1)}, u32[]{:S(2)}) copy-start(bf16[256,4,128]{2,1,0:T(4,128)(2,1)} %slice.323) | copy-start | bytes 786436
  145.5 22.5 %collective-permute-start.3 = (bf16[512,512]{1,0:T(8,128)(2,1)}, bf16[512,512]{1,0:T(8,128)(2,1)}, u32[]{:S(2)}, u32[]{:S(2)}) collective-permute-start(bf16[512,512]{1,0:T(8,128)(2,1)} %bitcast.233), channel_id=1, source_target_pairs={{0,1},{1,0},{2,3},{3,2},{4,5},{5,4},{6,7},{7,6},{8,9},{9,8},{10,11... | collective-permute-start | bytes 1572872 | tf_op jit(solution)/shard_map/ppermute | solution.py:10
  146.0 7.2 %copy-start.7 = (f32[4,128,256]{1,2,0:T(8,128)}, f32[4,128,256]{1,2,0:T(8,128)S(1)}, u32[]{:S(2)}) copy-start(f32[4,128,256]{1,2,0:T(8,128)S(1)} %convolution_bitcast_fusion.8) | copy-start | bytes 1572868
  148.5 4.7 %copy-start.4 = (bf16[256,4,128]{2,1,0:T(4,128)(2,1)S(1)}, bf16[256,4,128]{2,1,0:T(4,128)(2,1)}, u32[]{:S(2)}) copy-start(bf16[256,4,128]{2,1,0:T(4,128)(2,1)} %slice.315) | copy-start | bytes 786436
  148.5 4.7 %copy-start.10 = (bf16[128,4,128]{2,1,0:T(4,128)(2,1)S(1)}, bf16[128,4,128]{2,1,0:T(4,128)(2,1)}, u32[]{:S(2)}) copy-start(bf16[128,4,128]{2,1,0:T(4,128)(2,1)} %slice.317) | copy-start | bytes 393220
  153.2 3.8 %copy-start.8 = (bf16[128,4,128]{2,1,0:T(4,128)(2,1)S(1)}, bf16[128,4,128]{2,1,0:T(4,128)(2,1)}, u32[]{:S(2)}) copy-start(bf16[128,4,128]{2,1,0:T(4,128)(2,1)} %slice.309) | copy-start | bytes 393220
  154.2 3.0 %copy-start.16 = (bf16[256,4,128]{2,1,0:T(4,128)(2,1)S(1)}, bf16[256,4,128]{2,1,0:T(4,128)(2,1)}, u32[]{:S(2)}) copy-start(bf16[256,4,128]{2,1,0:T(4,128)(2,1)} %copy-done.15) | copy-start | bytes 786436
  156.9 1.9 copy-start.25
  157.0 1.9 copy-start.26
  157.2 1.7 copy-start.27
  158.9 1.5 copy-start.24
  160.3 5.0 %copy-start.23 = (bf16[128,4,128]{2,1,0:T(4,128)(2,1)S(1)}, bf16[128,4,128]{2,1,0:T(4,128)(2,1)}, u32[]{:S(2)}) copy-start(bf16[128,4,128]{2,1,0:T(4,128)(2,1)} %slice.313) | copy-start | bytes 393220
  162.7 5.4 %copy-start.1 = (f32[512,1,512]{2,1,0:T(1,128)S(1)}, f32[512,1,512]{2,1,0:T(1,128)}, u32[]{:S(2)}) copy-start(f32[512,1,512]{2,1,0:T(1,128)} %get-tuple-element.103) | copy-start | bytes 3145732
  170.1 36.5 %all-to-all-start.4 = ((bf16[8,64,1,512]{3,1,2,0:T(8,128)(2,1)}), bf16[8,64,1,512]{3,1,2,0:T(8,128)(2,1)}, u32[]{:S(2)}, u32[]{:S(2)}) async-start(bf16[8,64,1,512]{3,1,2,0:T(8,128)(2,1)} %bitcast.239), calls=%async_computation.4 | async-start | bytes 1048576 | tf_op jit(solution)/shard_map/all_to_all | solution.py:142
  174.9 72.1 %reduce-scatter.2.cloned.1.call-start = ((), (), s32[]{:S(2)}) async-start(), calls=%async_computation.9 | async-start | bytes 1310720 | tf_op jit(solution)/shard_map/reduce_scatter | solution.py:127
  184.4 3.3 %copy-start.22 = (bf16[128,4,128]{2,1,0:T(4,128)(2,1)S(1)}, bf16[128,4,128]{2,1,0:T(4,128)(2,1)}, u32[]{:S(2)}) copy-start(bf16[128,4,128]{2,1,0:T(4,128)(2,1)} %slice.321) | copy-start | bytes 393220
  185.6 4.9 %copy-start.20 = (bf16[128,4,128]{2,1,0:T(4,128)(2,1)S(1)}, bf16[128,4,128]{2,1,0:T(4,128)(2,1)}, u32[]{:S(2)}) copy-start(bf16[128,4,128]{2,1,0:T(4,128)(2,1)} %slice.329) | copy-start | bytes 393220
  185.6 17.1 %collective-permute-start.4 = (bf16[2048,256]{1,0:T(8,128)(2,1)}, bf16[2048,256]{1,0:T(8,128)(2,1)}, u32[]{:S(2)}, u32[]{:S(2)}) collective-permute-start(bf16[2048,256]{1,0:T(8,128)(2,1)} %fusion.61), channel_id=1, source_target_pairs={{0,1},{1,0},{2,3},{3,2},{4,5},{5,4},{6,7},{7,6},{8,9},{9,8},{10,11... | collective-permute-start | bytes 3145736 | tf_op jit(solution)/shard_map/ppermute | solution.py:10
  198.7 3.9 %copy-start = (f32[2048,1,256]{2,0,1:T(8,128)S(1)}, f32[2048,1,256]{2,0,1:T(8,128)}, u32[]{:S(2)}) copy-start(f32[2048,1,256]{2,0,1:T(8,128)} %copy.181) | copy-start | bytes 6291460
  202.7 2.8 %copy-start.2 = (f32[512,1,512]{2,1,0:T(1,128)S(1)}, f32[512,1,512]{2,1,0:T(1,128)}, u32[]{:S(2)}) copy-start(f32[512,1,512]{2,1,0:T(1,128)} %get-tuple-element.105) | copy-start | bytes 3145732
  202.7 2.8 %collective-permute-start.2 = (bf16[512,512]{1,0:T(8,128)(2,1)}, bf16[512,512]{1,0:T(8,128)(2,1)}, u32[]{:S(2)}, u32[]{:S(2)}) collective-permute-start(bf16[512,512]{1,0:T(8,128)(2,1)} %bitcast.234), channel_id=1, source_target_pairs={{0,1},{1,0},{2,3},{3,2},{4,5},{5,4},{6,7},{7,6},{8,9},{9,8},{10,11... | collective-permute-start | bytes 1572872 | tf_op jit(solution)/shard_map/ppermute | solution.py:10
  226.6 18.8 %all-to-all-start.6 = ((bf16[8,64,1,512]{3,1,2,0:T(8,128)(2,1)}), bf16[8,64,1,512]{3,1,2,0:T(8,128)(2,1)S(1)}, u32[]{:S(2)}, u32[]{:S(2)}) async-start(bf16[8,64,1,512]{3,1,2,0:T(8,128)(2,1)} %bitcast.60), calls=%async_computation.6 | async-start | bytes 1048576 | tf_op jit(solution)/shard_map/all_to_all | solution.py:144
Sparse Core Ops, SparseCore 0:
  205.5 28.9 reduce-scatter.1
where the time goes:
time: 258 us; the launch traced here: 256 us
  waiting for transfers between devices  62.4 us (24%)
  local copies, waits for them, and re-layouts  61.6 us (24%)
  matrix products  44 us (17%)
  starting transfers between devices  32.3 us (13%)
  other arithmetic  21 us (8%)
  blocking collectives  19.9 us (8%)
  between operations  14.5 us (6%)
    all_to_all x1, blocking collectives, body(): lax.all_to_all(to_tokens(key_grad), 'seq', split_axis=0, concat_axis=2, t...  19.9 us
    all_to_all x1, waiting for transfers between devices, body(): lax.all_to_all(to_heads(values), 'seq', split_axis=1, concat_axis=0, tile...  14 us
    all_to_all x1, waiting for transfers between devices, body(): lax.all_to_all(to_heads(out_grad), 'seq', split_axis=1, concat_axis=0, ti...  13.9 us
    all_to_all x1, waiting for transfers between devices, body(): lax.all_to_all(to_heads(key_vectors), 'seq', split_axis=1, concat_axis=0,...  13.2 us
    dot_general x4, matrix products, body(): jnp.einsum('hqk,qhd->khd', dscore, query_block, preferred_element_type=jn...  10.8 us
    all_to_all x1, waiting for transfers between devices, body(): lax.all_to_all(to_tokens(value_grad), 'seq', split_axis=0, concat_axis=2,...  10.8 us
    all_to_all x1, waiting for transfers between devices, body(): lax.all_to_all(to_heads(queries), 'seq', split_axis=1, concat_axis=0, til...  10.3 us
    dot_general x4, matrix products, body(): jnp.einsum('hqk,qhd->khd', probs_low, grad_block, preferred_element_type=...  9.58 us
  transfers between devices with their start and end apart: 13, of which 5 were waited for; matrix products, arithmetic and copies ran while one was open for 48% of the time, Pallas kernels for 0%

commit v1 on v0

--- a/solution.py
+++ b/solution.py
@@ -4,6 +4,29 @@
 from jax.sharding import PartitionSpec as P
 
 HD = 128
+
+
+def in_blocks(array, dim, count):
+    before, after = (array.shape[:dim], array.shape[dim + 1 :])
+    return jnp.moveaxis(array.reshape(*before, count, -1, *after), dim, 0)
+
+
+def joined_along(blocks, dim):
+    shape = list(blocks.shape[1:])
+    shape[dim] *= blocks.shape[0]
+    return jnp.moveaxis(blocks, 0, dim).reshape(shape)
+
+
+def rotated_exchange(x, axis, split_dim, concat_dim):
+    length, place = (lax.axis_size(axis), lax.axis_index(axis))
+    blocks = in_blocks(x, split_dim, length)
+    whole = blocks
+    for step in range(1, length):
+        target, source = ((place + step) % length, (place - step) % length)
+        sent = lax.dynamic_index_in_dim(blocks, target, 0)
+        partner_block = lax.ppermute(sent, axis, [(i, (i + step) % length) for i in range(length)])
+        whole = lax.dynamic_update_slice_in_dim(whole, partner_block, source, axis=0)
+    return joined_along(whole, concat_dim)
 
 
 def partner(value, axis, apart):
@@ -40,7 +63,7 @@
         lax.all_to_all(to_heads(queries), "seq", split_axis=1, concat_axis=0, tiled=True),
         lax.all_to_all(to_heads(key_vectors), "seq", split_axis=1, concat_axis=0, tiled=True),
         lax.all_to_all(to_heads(values), "seq", split_axis=1, concat_axis=0, tiled=True),
-        lax.all_to_all(to_heads(out_grad), "seq", split_axis=1, concat_axis=0, tiled=True),
+        rotated_exchange(to_heads(out_grad), "seq", 1, 0),
     )
     q_rows = moved[0].reshape(own_rows, group_width)
     k_rows = moved[1].reshape(own_rows, group_width)

time: 258 us -> 239 us (0.926)
  waiting for transfers between devices: 62.4 us -> 41.7 us
  starting transfers between devices: 32.3 us -> 40.2 us
  local copies, waits for them, and re-layouts: 61.6 us -> 56.7 us
    all_to_all x1 -> x0, waiting for transfers between devices: 13.9 us -> none  [body(): lax.all_to_all(to_heads(out_grad), 'seq', split_axis=1, concat_axis=0, ti...]
    ppermute x0 -> x7, starting transfers between devices: none -> 10.8 us  [rotated_exchange(): lax.ppermute(sent, axis, [(i, (i + step) % length) for i in range(length)])]
    all_to_all x1, waiting for transfers between devices: 13.2 us -> 7.88 us  [body(): lax.all_to_all(to_heads(key_vectors), 'seq', split_axis=1, concat_axis=0,...]
    all_to_all x1 -> x0, starting transfers between devices: 3.63 us -> none  [body(): lax.all_to_all(to_heads(out_grad), 'seq', split_axis=1, concat_axis=0, ti...]
    all_to_all x1, waiting for transfers between devices: 14 us -> 11.1 us  [body(): lax.all_to_all(to_heads(values), 'seq', split_axis=1, concat_axis=0, tile...]
  transfers between devices with their start and end apart: 13 -> 19, of which waited for: 5 -> 4; matrix products, arithmetic and copies ran while one was open for 48% -> 49% of each run, Pallas kernels for 0% -> 0%
where the time goes in v1:
time: 239 us; the launch traced here: 238 us
  local copies, waits for them, and re-layouts  56.7 us (24%)
  matrix products  43.3 us (18%)
  waiting for transfers between devices  41.7 us (17%)
  starting transfers between devices  40.2 us (17%)
  other arithmetic  21 us (9%)
  blocking collectives  19.9 us (8%)
  between operations  14.7 us (6%)
    all_to_all x1, blocking collectives, body(): lax.all_to_all(to_tokens(key_grad), 'seq', split_axis=0, concat_axis=2, t...  19.9 us
    all_to_all x1, waiting for transfers between devices, body(): lax.all_to_all(to_heads(queries), 'seq', split_axis=1, concat_axis=0, til...  11.9 us
    all_to_all x1, waiting for transfers between devices, body(): lax.all_to_all(to_heads(values), 'seq', split_axis=1, concat_axis=0, tile...  11.1 us
    all_to_all x1, waiting for transfers between devices, body(): lax.all_to_all(to_tokens(value_grad), 'seq', split_axis=0, concat_axis=2,...  10.8 us
    ppermute x7, starting transfers between devices, rotated_exchange(): lax.ppermute(sent, axis, [(i, (i + step) % length) for i in range(length)])  10.8 us
    dot_general x4, matrix products, body(): jnp.einsum('hqk,qhd->khd', dscore, query_block, preferred_element_type=jn...  10.7 us
    dot_general x4, matrix products, body(): jnp.einsum('hqk,qhd->khd', probs_low, grad_block, preferred_element_type=...  9.76 us
    dot_general x4, matrix products, body(): jnp.einsum('hqk,khd->qhd', dscore, key_block, preferred_element_type=jnp....  8.84 us
  transfers between devices with their start and end apart: 19, of which 4 were waited for; matrix products, arithmetic and copies ran while one was open for 49% of the time, Pallas kernels for 0%

profile of v1, /device:TPU:0, one launch (start us, length us, event | category | flops | bytes accessed | tf_op | source)
XLA Modules:
  0.0 237.6 jit_solution(8235667664040158257)
XLA Ops:
  9.6 6.5 %all-to-all-start.2 = ((bf16[64,8,512]{2,0,1:T(8,128)(2,1)}), bf16[64,8,512]{2,0,1:T(8,128)(2,1)S(1)}, u32[]{:S(2)}, u32[]{:S(2)}) async-start(bf16[64,8,512]{2,0,1:T(8,128)(2,1)} %bitcast.25), calls=%async_computation.2 | async-start | bytes 1048576 | tf_op jit(solution)/shard_map/all_to_all | solution.py:65
  17.9 1.7 collective-permute-start.2
  19.6 2.2 collective-permute-start.3
  26.4 11.1 %all-to-all-done.2 = bf16[64,8,512]{2,0,1:T(8,128)(2,1)S(1)} async-done(((bf16[64,8,512]{2,0,1:T(8,128)(2,1)}), bf16[64,8,512]{2,0,1:T(8,128)(2,1)S(1)}, u32[]{:S(2)}, u32[]{:S(2)}) %all-to-all-start.2) | async-done | bytes 524320 | tf_op jit(solution)/shard_map/all_to_all | solution.py:65
  37.5 3.5 %all-to-all-start = ((bf16[64,8,512]{2,0,1:T(8,128)(2,1)}), bf16[64,8,512]{2,0,1:T(8,128)(2,1)S(1)}, u32[]{:S(2)}, u32[]{:S(2)}) async-start(bf16[64,8,512]{2,0,1:T(8,128)(2,1)} %bitcast.1), calls=%async_computation | async-start | bytes 1048576 | tf_op jit(solution)/shard_map/all_to_all | solution.py:64
  45.0 3.8 %collective-permute-start.6 = (bf16[1,64,1,512]{3,1,0,2:T(8,128)(2,1)}, bf16[1,64,1,512]{3,1,0,2:T(8,128)(2,1)S(1)}, u32[]{:S(2)}, u32[]{:S(2)}) collective-permute-start(bf16[1,64,1,512]{3,1,0,2:T(8,128)(2,1)} %get-tuple-element.127), channel_id=1, source_target_pairs={{0,6},{1,7},{2,0},{3,1},{4,2},{5,3},{6,4},{7,5},{8,14},{9,15},{10,... | collective-permute-start | bytes 196616 | tf_op jit(solution)/shard_map/ppermute | solution.py:27
  48.9 7.9 %all-to-all-done = bf16[64,8,512]{2,0,1:T(8,128)(2,1)S(1)} async-done(((bf16[64,8,512]{2,0,1:T(8,128)(2,1)}), bf16[64,8,512]{2,0,1:T(8,128)(2,1)S(1)}, u32[]{:S(2)}, u32[]{:S(2)}) %all-to-all-start) | async-done | bytes 524320 | tf_op jit(solution)/shard_map/all_to_all | solution.py:64
  56.8 4.2 %all-to-all-start.1 = ((bf16[64,8,512]{2,0,1:T(8,128)(2,1)}), bf16[64,8,512]{2,0,1:T(8,128)(2,1)S(1)}, u32[]{:S(2)}, u32[]{:S(2)}) async-start(bf16[64,8,512]{2,0,1:T(8,128)(2,1)} %bitcast.10), calls=%async_computation.1 | async-start | bytes 1048576 | tf_op jit(solution)/shard_map/all_to_all | solution.py:63
  64.4 11.9 %all-to-all-done.1 = bf16[64,8,512]{2,0,1:T(8,128)(2,1)S(1)} async-done(((bf16[64,8,512]{2,0,1:T(8,128)(2,1)}), bf16[64,8,512]{2,0,1:T(8,128)(2,1)S(1)}, u32[]{:S(2)}, u32[]{:S(2)}) %all-to-all-start.1) | async-done | bytes 524320 | tf_op jit(solution)/shard_map/all_to_all | solution.py:63
  76.3 1.6 broadcast_in_dim.67
  77.9 3.8 %all-to-all-start.6 = ((bf16[64,8,2048]{2,0,1:T(8,128)(2,1)}), bf16[64,8,2048]{2,0,1:T(8,128)(2,1)S(1)}, u32[]{:S(2)}, u32[]{:S(2)}) async-start(bf16[64,8,2048]{2,0,1:T(8,128)(2,1)} %bitcast.66), calls=%async_computation.6 | async-start | bytes 4194304 | tf_op jit(solution)/shard_map/all_to_all | solution.py:141
  81.7 1.8 fusion.215
  83.5 1.6 slice.329
  93.7 2.1 fusion.232
  95.8 2.3 convolution_bitcast_fusion.3
  98.1 2.6 %scatter-add.34 = f32[1024,4,128]{0,2,1:T(8,128)} pad(f32[256,4,128]{0,2,1:T(8,128)} %convolution_bitcast_fusion.3, f32[]{:T(128)} %constant.305.clone.1), padding=0_768x0_0x0_0 | pad | bytes 2621444 | tf_op jit(solution)/shard_map/scatter-add | solution.py:120
  100.7 2.1 fusion.217
  102.8 2.2 fusion.227
  105.0 2.4 %fusion.17 = f32[1024,4,128]{0,2,1:T(8,128)} fusion(f32[1024,4,128]{0,2,1:T(8,128)} %scatter-add.34, bf16[128,4,128]{0,2,1:T(8,128)(2,1)S(1)} %copy-done.8, f32[4,128]{1,0:T(4,128)S(1)} %get-tuple-element.137, pred[128,256]{0,1:T(8,128)(4,1)} %broadcast_compare_fusion.2, bf16[256,4,128]{2,1,0:T(4,128)(2,1)} %slice.311, bf16[128,4,128]{2,1,0:T(4,128)(2,1)} %slice.313), kind=kOutput, calls=%fused_computation.38 | convolution fusion | flops 67764992 | bytes 1083392 | tf_op jit(solution)/shard_map/hqk,qhd->khd/dot_general | solution.py:121
  107.9 1.9 fusion.222
  109.8 2.4 %fusion.24 = f32[1024,4,128]{0,2,1:T(8,128)} fusion(f32[1024,4,128]{0,2,1:T(8,128)} %fusion.17, bf16[128,4,128]{0,2,1:T(8,128)(2,1)S(1)} %copy-done.10, f32[4,128]{1,0:T(4,128)S(1)} %get-tuple-element.135, pred[128,256]{0,1:T(8,128)(4,1)} %broadcast_compare_fusion.1, bf16[256,4,128]{2,1,0:T(4,128)(2,1)S(1)} %slice.319, bf16[128,4,128]{2,1,0:T(4,128)(2,1)S(1)} %copy-done.22), kind=kOutput, calls=%fused_computation.50 | convolution fusion | flops 67896064 | bytes 1607680 | tf_op jit(solution)/shard_map/hqk,qhd->khd/dot_general | solution.py:121
  117.4 2.6 %fusion.26 = f32[1024,4,128]{0,2,1:T(8,128)} fusion(f32[1024,4,128]{0,2,1:T(8,128)} %fusion.24, bf16[128,4,128]{0,2,1:T(8,128)(2,1)} %copy.221, f32[4,128]{1,0:T(4,128)S(1)} %get-tuple-element.133, pred[128,256]{0,1:T(8,128)(4,1)} %broadcast_compare_fusion, bf16[256,4,128]{2,1,0:T(4,128)(2,1)} %slice.327, bf16[128,4,128]{2,1,0:T(4,128)(2,1)} %slice.329), kind=kOutput, calls=%fused_computation.52 | convolution fusion | flops 67896064 | bytes 1607680 | tf_op jit(solution)/shard_map/hqk,qhd->khd/dot_general | solution.py:121
  120.0 2.8 %copy.223 = bf16[1024,4,128]{2,1,0:T(4,128)(2,1)} copy(f32[1024,4,128]{0,2,1:T(8,128)} %fusion.26) | data formatting | bytes 3145728 | tf_op jit(solution)/shard_map/scatter-add | solution.py:120
  124.3 3.0 %fusion.60 = (bf16[512,1,512]{2,1,0:T(2,128)(2,1)S(1)}, f32[512,1,512]{2,1,0:T(1,128)}) fusion(pred[]{:T(512)S(6)} %eq.19, bf16[512,2,512]{2,1,0:T(2,128)(2,1)S(1)} %reshape.500), kind=kLoop, calls=%fused_computation.94 | loop fusion | flops 786432 | bytes 2621441 | tf_op jit(solution)/shard_map/convert_element_type | solution.py:129
  128.7 2.4 %fusion.54 = bf16[128,4,128]{2,0,1:T(8,128)(2,1)} fusion(f32[4,128,256]{1,2,0:T(8,128)S(1)} %fusion.86, bf16[256,4,128]{2,1,0:T(4,128)(2,1)S(1)} %copy-done.18, f32[4,128,256]{1,2,0:T(8,128)} %get-tuple-element.134, f32[4,128]{1,0:T(4,128)S(1)} %get-tuple-element.133), kind=kOutput, calls=%fused_computation.88 | convolution fusion | flops 34538240 | bytes 1443840 | tf_op jit(solution)/shard_map/hqk,khd->qhd/dot_general | solution.py:113
  131.2 2.0 fusion.88
  133.1 2.0 fusion.53
  136.2 2.8 %fusion.52 = bf16[128,4,128]{2,0,1:T(8,128)(2,1)} fusion(f32[4,128,256]{1,2,0:T(8,128)} %fusion.90, bf16[256,4,128]{2,1,0:T(4,128)(2,1)} %slice.311, f32[4,128,256]{1,2,0:T(8,128)} %get-tuple-element.138, f32[4,128]{1,0:T(4,128)S(1)} %get-tuple-element.137), kind=kOutput, calls=%fused_computation.86 | convolution fusion | flops 34538240 | bytes 1443840 | tf_op jit(solution)/shard_map/hqk,khd->qhd/dot_general | solution.py:113
  139.2 1.6 fusion.51
  142.3 2.4 convolution_bitcast_fusion.7
  144.7 2.6 %scatter-add.26 = f32[1024,4,128]{2,0,1:T(8,128)} pad(f32[256,4,128]{2,0,1:T(8,128)} %convolution_bitcast_fusion.7, f32[]{:T(128)} %constant.305.clone.1), padding=0_768x0_0x0_0 | pad | bytes 2621444 | tf_op jit(solution)/shard_map/scatter-add | solution.py:117
  147.2 2.8 %fusion.18 = f32[1024,4,128]{2,0,1:T(8,128)} fusion(f32[1024,4,128]{2,0,1:T(8,128)} %scatter-add.26, f32[4,128,256]{1,2,0:T(8,128)} %fusion.90, bf16[128,4,128]{2,1,0:T(4,128)(2,1)S(1)} %copy-done.24, f32[4,128,256]{1,2,0:T(8,128)} %get-tuple-element.138, f32[4,128]{1,0:T(4,128)S(1)} %get-tuple-element.137), kind=kOutput, calls=%fused_computation.43 | convolution fusion | flops 34472704 | bytes 2756608 | tf_op jit(solution)/shard_map/hqk,qhd->khd/dot_general | solution.py:118
  150.0 2.1 fusion.62
  152.1 4.8 %all-to-all-start.3 = ((bf16[8,64,1,512]{3,1,2,0:T(8,128)(2,1)}), bf16[8,64,1,512]{3,1,2,0:T(8,128)(2,1)}, u32[]{:S(2)}, u32[]{:S(2)}) async-start(bf16[8,64,1,512]{3,1,2,0:T(8,128)(2,1)} %bitcast.254), calls=%async_computation.3 | async-start | bytes 1048576 | tf_op jit(solution)/shard_map/all_to_all | solution.py:165
  156.9 2.3 fusion.237
  159.3 2.2 fusion.214
  161.5 1.9 copy.246
  163.4 2.9 %copy.245 = f32[2048,1,256]{2,0,1:T(8,128)} copy(f32[2048,1,256]{0,2,1:T(8,128)} %get-tuple-element.100) | data formatting | bytes 4194304
  167.6 2.1 collective-permute-start.11
  169.7 2.8 %fusion.20 = f32[1024,4,128]{2,0,1:T(8,128)} fusion(f32[1024,4,128]{2,0,1:T(8,128)} %fusion.18, f32[4,128,256]{1,2,0:T(8,128)} %fusion.88, bf16[128,4,128]{2,1,0:T(4,128)(2,1)S(1)} %copy-done.23, f32[4,128,256]{1,2,0:T(8,128)} %get-tuple-element.136, f32[4,128]{1,0:T(4,128)S(1)} %get-tuple-element.135), kind=kOutput, calls=%fused_computation.46 | convolution fusion | flops 34603776 | bytes 3280896 | tf_op jit(solution)/shard_map/hqk,qhd->khd/dot_general | solution.py:118
  172.5 2.8 %fusion.22 = f32[1024,4,128]{2,0,1:T(8,128)} fusion(f32[1024,4,128]{2,0,1:T(8,128)} %fusion.20, f32[4,128,256]{1,2,0:T(8,128)} %copy-done.7, bf16[128,4,128]{2,1,0:T(4,128)(2,1)S(1)} %copy-done.21, f32[4,128,256]{1,2,0:T(8,128)} %get-tuple-element.134, f32[4,128]{1,0:T(4,128)S(1)} %get-tuple-element.133), kind=kOutput, calls=%fused_computation.48 | convolution fusion | flops 34603776 | bytes 3280896 | tf_op jit(solution)/shard_map/hqk,qhd->khd/dot_general | solution.py:118
  175.3 3.9 %copy.212 = bf16[1024,4,128]{2,1,0:T(4,128)(2,1)} copy(f32[1024,4,128]{2,0,1:T(8,128)} %fusion.22) | data formatting | bytes 3145728 | tf_op jit(solution)/shard_map/scatter-add | solution.py:117
  180.7 3.0 %fusion.57 = (bf16[512,1,512]{2,1,0:T(2,128)(2,1)S(1)}, f32[512,1,512]{2,1,0:T(1,128)}) fusion(pred[]{:T(512)S(6)} %eq.19, bf16[512,2,512]{2,1,0:T(2,128)(2,1)S(1)} %reshape.496), kind=kLoop, calls=%fused_computation.91 | loop fusion | flops 786432 | bytes 2621441 | tf_op jit(solution)/shard_map/convert_element_type | solution.py:129
  184.7 2.7 %fusion.8 = bf16[2048,256]{1,0:T(8,128)(2,1)} fusion(bf16[2048,256]{1,0:T(8,128)(2,1)} %collective-permute-done.11, f32[2048,1,256]{2,0,1:T(8,128)S(1)} %copy-done, f32[2048,1,256]{2,0,1:T(8,128)S(1)} %copy.246, pred[]{:T(512)S(6)} %eq.19), kind=kLoop, calls=%fused_computation.9 | loop fusion | flops 2097152 | bytes 6291457 | tf_op jit(solution)/shard_map/convert_element_type | solution.py:151
  188.7 19.9 %all_to_all.105 = bf16[8,64,1,512]{3,1,2,0:T(8,128)(2,1)S(1)} all-to-all(bf16[8,64,1,512]{3,1,2,0:T(8,128)(2,1)S(1)} %bitcast.262), channel_id=1, replica_groups=mesh['dp'=4,'seq'=8] {'seq'}, dimensions={0} | all-to-all | bytes 1048576 | tf_op jit(solution)/shard_map/all_to_all | solution.py:166
  208.6 3.8 %all-to-all-start.5 = ((bf16[8,64,1,512]{3,1,2,0:T(8,128)(2,1)}), bf16[8,64,1,512]{3,1,2,0:T(8,128)(2,1)S(1)}, u32[]{:S(2)}, u32[]{:S(2)}) async-start(bf16[8,64,1,512]{3,1,2,0:T(8,128)(2,1)} %bitcast.61), calls=%async_computation.5 | async-start | bytes 1048576 | tf_op jit(solution)/shard_map/all_to_all | solution.py:167
  216.6 10.8 %all-to-all-done.5 = bf16[8,64,1,512]{3,1,2,0:T(8,128)(2,1)S(1)} async-done(((bf16[8,64,1,512]{3,1,2,0:T(8,128)(2,1)}), bf16[8,64,1,512]{3,1,2,0:T(8,128)(2,1)S(1)}, u32[]{:S(2)}, u32[]{:S(2)}) %all-to-all-start.5) | async-done | bytes 524320 | tf_op jit(solution)/shard_map/all_to_all | solution.py:167
  229.0 1.8 convert_element_type.141
  (158 shorter events, 46.6 us)
Async XLA Ops:
  7.2 8.9 %copy-start.12 = (bf16[1,128,2048]{2,1,0:T(8,128)(2,1)S(1)}, bf16[1,128,2048]{2,1,0:T(8,128)(2,1)}, u32[]{:S(2)}) copy-start(bf16[1,128,2048]{2,1,0:T(8,128)(2,1)} %param.24) | copy-start | bytes 1572868
  9.6 14.7 %copy-start.13 = (bf16[1,128,2048]{2,1,0:T(8,128)(2,1)S(1)}, bf16[1,128,2048]{2,1,0:T(8,128)(2,1)}, u32[]{:S(2)}) copy-start(bf16[1,128,2048]{2,1,0:T(8,128)(2,1)} %param.22) | copy-start | bytes 1572868
  9.6 27.9 %all-to-all-start.2 = ((bf16[64,8,512]{2,0,1:T(8,128)(2,1)}), bf16[64,8,512]{2,0,1:T(8,128)(2,1)S(1)}, u32[]{:S(2)}, u32[]{:S(2)}) async-start(bf16[64,8,512]{2,0,1:T(8,128)(2,1)} %bitcast.25), calls=%async_computation.2 | async-start | bytes 1048576 | tf_op jit(solution)/shard_map/all_to_all | solution.py:65
  16.7 26.5 %copy-start.14 = (bf16[1,128,2048]{2,1,0:T(8,128)(2,1)S(1)}, bf16[1,128,2048]{2,1,0:T(8,128)(2,1)}, u32[]{:S(2)}) copy-start(bf16[1,128,2048]{2,1,0:T(8,128)(2,1)} %param.21) | copy-start | bytes 1572868
  17.4 27.6 %collective-permute-start.1 = (bf16[1,64,1,512]{3,1,0,2:T(8,128)(2,1)}, bf16[1,64,1,512]{3,1,0,2:T(8,128)(2,1)S(1)}, u32[]{:S(2)}, u32[]{:S(2)}) collective-permute-start(bf16[1,64,1,512]{3,1,0,2:T(8,128)(2,1)} %get-tuple-element.132), channel_id=1, source_target_pairs={{0,1},{1,2},{2,3},{3,4},{4,5},{5,6},{6,7},{7,0},{8,9},{9,10},{10,1... | collective-permute-start | bytes 196616 | tf_op jit(solution)/shard_map/ppermute | solution.py:27
  17.9 30.9 %collective-permute-start.2 = (bf16[1,64,1,512]{3,1,0,2:T(8,128)(2,1)}, bf16[1,64,1,512]{3,1,0,2:T(8,128)(2,1)S(1)}, u32[]{:S(2)}, u32[]{:S(2)}) collective-permute-start(bf16[1,64,1,512]{3,1,0,2:T(8,128)(2,1)} %get-tuple-element.131), channel_id=1, source_target_pairs={{0,2},{1,3},{2,4},{3,5},{4,6},{5,7},{6,0},{7,1},{8,10},{9,11},{10,... | collective-permute-start | bytes 196616 | tf_op jit(solution)/shard_map/ppermute | solution.py:27
  19.6 41.4 %collective-permute-start.3 = (bf16[1,64,1,512]{3,1,0,2:T(8,128)(2,1)}, bf16[1,64,1,512]{3,1,0,2:T(8,128)(2,1)S(1)}, u32[]{:S(2)}, u32[]{:S(2)}) collective-permute-start(bf16[1,64,1,512]{3,1,0,2:T(8,128)(2,1)} %get-tuple-element.130), channel_id=1, source_target_pairs={{0,3},{1,4},{2,5},{3,6},{4,7},{5,0},{6,1},{7,2},{8,11},{9,12},{10,... | collective-permute-start | bytes 196616 | tf_op jit(solution)/shard_map/ppermute | solution.py:27
  21.8 39.2 %collective-permute-start.4 = (bf16[1,64,1,512]{3,1,0,2:T(8,128)(2,1)}, bf16[1,64,1,512]{3,1,0,2:T(8,128)(2,1)S(1)}, u32[]{:S(2)}, u32[]{:S(2)}) collective-permute-start(bf16[1,64,1,512]{3,1,0,2:T(8,128)(2,1)} %get-tuple-element.129), channel_id=1, source_target_pairs={{0,4},{1,5},{2,6},{3,7},{4,0},{5,1},{6,2},{7,3},{8,12},{9,13},{10,... | collective-permute-start | bytes 196616 | tf_op jit(solution)/shard_map/ppermute | solution.py:27
  23.3 37.7 %collective-permute-start.5 = (bf16[1,64,1,512]{3,1,0,2:T(8,128)(2,1)}, bf16[1,64,1,512]{3,1,0,2:T(8,128)(2,1)S(1)}, u32[]{:S(2)}, u32[]{:S(2)}) collective-permute-start(bf16[1,64,1,512]{3,1,0,2:T(8,128)(2,1)} %get-tuple-element.128), channel_id=1, source_target_pairs={{0,5},{1,6},{2,7},{3,0},{4,1},{5,2},{6,3},{7,4},{8,13},{9,14},{10,... | collective-permute-start | bytes 196616 | tf_op jit(solution)/shard_map/ppermute | solution.py:27
  24.7 19.8 %copy-start.15 = (bf16[1,128,2048]{2,1,0:T(8,128)(2,1)S(1)}, bf16[1,128,2048]{2,1,0:T(8,128)(2,1)}, u32[]{:S(2)}) copy-start(bf16[1,128,2048]{2,1,0:T(8,128)(2,1)} %param.25) | copy-start | bytes 1572868
  37.5 19.3 %all-to-all-start = ((bf16[64,8,512]{2,0,1:T(8,128)(2,1)}), bf16[64,8,512]{2,0,1:T(8,128)(2,1)S(1)}, u32[]{:S(2)}, u32[]{:S(2)}) async-start(bf16[64,8,512]{2,0,1:T(8,128)(2,1)} %bitcast.1), calls=%async_computation | async-start | bytes 1048576 | tf_op jit(solution)/shard_map/all_to_all | solution.py:64
  45.0 16.0 %collective-permute-start.6 = (bf16[1,64,1,512]{3,1,0,2:T(8,128)(2,1)}, bf16[1,64,1,512]{3,1,0,2:T(8,128)(2,1)S(1)}, u32[]{:S(2)}, u32[]{:S(2)}) collective-permute-start(bf16[1,64,1,512]{3,1,0,2:T(8,128)(2,1)} %get-tuple-element.127), channel_id=1, source_target_pairs={{0,6},{1,7},{2,0},{3,1},{4,2},{5,3},{6,4},{7,5},{8,14},{9,15},{10,... | collective-permute-start | bytes 196616 | tf_op jit(solution)/shard_map/ppermute | solution.py:27
  48.8 12.8 %collective-permute-start.7 = (bf16[1,64,1,512]{3,1,0,2:T(8,128)(2,1)S(1)}, bf16[1,64,1,512]{3,1,0,2:T(8,128)(2,1)S(1)}, u32[]{:S(2)}, u32[]{:S(2)}) collective-permute-start(bf16[1,64,1,512]{3,1,0,2:T(8,128)(2,1)S(1)} %get-tuple-element.126), channel_id=1, source_target_pairs={{0,7},{1,0},{2,1},{3,2},{4,3},{5,4},{6,5},{7,6},{8,15},{9,8},{10,9... | collective-permute-start | bytes 196616 | tf_op jit(solution)/shard_map/ppermute | solution.py:27
  56.8 19.5 %all-to-all-start.1 = ((bf16[64,8,512]{2,0,1:T(8,128)(2,1)}), bf16[64,8,512]{2,0,1:T(8,128)(2,1)S(1)}, u32[]{:S(2)}, u32[]{:S(2)}) async-start(bf16[64,8,512]{2,0,1:T(8,128)(2,1)} %bitcast.10), calls=%async_computation.1 | async-start | bytes 1048576 | tf_op jit(solution)/shard_map/all_to_all | solution.py:63
  61.1 27.1 %collective-permute-start = (bf16[512,512]{1,0:T(8,128)(2,1)S(1)}, bf16[512,512]{1,0:T(8,128)(2,1)}, u32[]{:S(2)}, u32[]{:S(2)}) collective-permute-start(bf16[512,512]{1,0:T(8,128)(2,1)S(1)} %bitcast.253), channel_id=1, source_target_pairs={{0,1},{1,0},{2,3},{3,2},{4,5},{5,4},{6,7},{7,6},{8,9},{9,8},{10,11... | collective-permute-start | bytes 1572872 | tf_op jit(solution)/shard_map/ppermute | solution.py:33
  64.3 47.9 %collective-permute-start.8 = (bf16[512,512]{1,0:T(8,128)(2,1)S(1)}, bf16[512,512]{1,0:T(8,128)(2,1)}, u32[]{:S(2)}, u32[]{:S(2)}) collective-permute-start(bf16[512,512]{1,0:T(8,128)(2,1)S(1)} %bitcast.252), channel_id=1, source_target_pairs={{0,1},{1,0},{2,3},{3,2},{4,5},{5,4},{6,7},{7,6},{8,9},{9,8},{10,11... | collective-permute-start | bytes 1572872 | tf_op jit(solution)/shard_map/ppermute | solution.py:33
  76.3 1.6 copy-start.3
  77.9 74.2 %all-to-all-start.6 = ((bf16[64,8,2048]{2,0,1:T(8,128)(2,1)}), bf16[64,8,2048]{2,0,1:T(8,128)(2,1)S(1)}, u32[]{:S(2)}, u32[]{:S(2)}) async-start(bf16[64,8,2048]{2,0,1:T(8,128)(2,1)} %bitcast.66), calls=%async_computation.6 | async-start | bytes 4194304 | tf_op jit(solution)/shard_map/all_to_all | solution.py:141
  93.7 7.0 %copy-start.16 = (bf16[256,4,128]{2,1,0:T(4,128)(2,1)}, bf16[256,4,128]{2,1,0:T(4,128)(2,1)S(1)}, u32[]{:S(2)}) copy-start(bf16[256,4,128]{2,1,0:T(4,128)(2,1)S(1)} %slice.303) | copy-start | bytes 786436
  95.8 4.9 %copy-start.20 = (bf16[128,4,128]{2,1,0:T(4,128)(2,1)S(1)}, bf16[128,4,128]{2,1,0:T(4,128)(2,1)}, u32[]{:S(2)}) copy-start(bf16[128,4,128]{2,1,0:T(4,128)(2,1)} %slice.329) | copy-start | bytes 393220
  100.7 4.3 %copy-start.8 = (bf16[128,4,128]{0,2,1:T(8,128)(2,1)S(1)}, bf16[128,4,128]{0,2,1:T(8,128)(2,1)}, u32[]{:S(2)}) copy-start(bf16[128,4,128]{0,2,1:T(8,128)(2,1)} %copy.217) | copy-start | bytes 393220
  105.0 2.9 %copy-start.22 = (bf16[128,4,128]{2,1,0:T(4,128)(2,1)S(1)}, bf16[128,4,128]{2,1,0:T(4,128)(2,1)}, u32[]{:S(2)}) copy-start(bf16[128,4,128]{2,1,0:T(4,128)(2,1)} %slice.321) | copy-start | bytes 393220
  105.0 4.8 %copy-start.10 = (bf16[128,4,128]{0,2,1:T(8,128)(2,1)S(1)}, bf16[128,4,128]{0,2,1:T(8,128)(2,1)}, u32[]{:S(2)}) copy-start(bf16[128,4,128]{0,2,1:T(8,128)(2,1)} %copy.219) | copy-start | bytes 393220
  107.9 4.3 %copy-start.19 = (bf16[256,4,128]{2,1,0:T(4,128)(2,1)}, bf16[256,4,128]{2,1,0:T(4,128)(2,1)S(1)}, u32[]{:S(2)}) copy-start(bf16[256,4,128]{2,1,0:T(4,128)(2,1)S(1)} %slice.319) | copy-start | bytes 786436
  124.3 4.2 %copy-start.6 = (bf16[256,4,128]{2,1,0:T(4,128)(2,1)S(1)}, bf16[256,4,128]{2,1,0:T(4,128)(2,1)}, u32[]{:S(2)}) copy-start(bf16[256,4,128]{2,1,0:T(4,128)(2,1)} %slice.333) | copy-start | bytes 786436
  124.3 4.2 %copy-start.11 = (bf16[128,4,128]{0,2,1:T(8,128)(2,1)S(1)}, bf16[128,4,128]{0,2,1:T(8,128)(2,1)}, u32[]{:S(2)}) copy-start(bf16[128,4,128]{0,2,1:T(8,128)(2,1)} %copy.221) | copy-start | bytes 393220
  127.3 1.4 copy-start.18
  128.3 2.9 %copy-start.5 = (bf16[256,4,128]{2,1,0:T(4,128)(2,1)S(1)}, bf16[256,4,128]{2,1,0:T(4,128)(2,1)}, u32[]{:S(2)}) copy-start(bf16[256,4,128]{2,1,0:T(4,128)(2,1)} %slice.325) | copy-start | bytes 786436
  128.3 21.7 %collective-permute-start.10 = (bf16[512,512]{1,0:T(8,128)(2,1)}, bf16[512,512]{1,0:T(8,128)(2,1)}, u32[]{:S(2)}, u32[]{:S(2)}) collective-permute-start(bf16[512,512]{1,0:T(8,128)(2,1)} %bitcast.246), channel_id=1, source_target_pairs={{0,1},{1,0},{2,3},{3,2},{4,5},{5,4},{6,7},{7,6},{8,9},{9,8},{10,11... | collective-permute-start | bytes 1572872 | tf_op jit(solution)/shard_map/ppermute | solution.py:33
  128.7 6.5 %copy-start.7 = (f32[4,128,256]{1,2,0:T(8,128)}, f32[4,128,256]{1,2,0:T(8,128)S(1)}, u32[]{:S(2)}) copy-start(f32[4,128,256]{1,2,0:T(8,128)S(1)} %fusion.86) | copy-start | bytes 1572868
  131.2 4.0 %copy-start.4 = (bf16[256,4,128]{2,1,0:T(4,128)(2,1)S(1)}, bf16[256,4,128]{2,1,0:T(4,128)(2,1)}, u32[]{:S(2)}) copy-start(bf16[256,4,128]{2,1,0:T(4,128)(2,1)} %slice.317) | copy-start | bytes 786436
  133.1 2.1 copy-start.9
  136.2 3.0 %copy-start.17 = (bf16[256,4,128]{2,1,0:T(4,128)(2,1)S(1)}, bf16[256,4,128]{2,1,0:T(4,128)(2,1)}, u32[]{:S(2)}) copy-start(bf16[256,4,128]{2,1,0:T(4,128)(2,1)} %copy-done.16) | copy-start | bytes 786436
  139.0 1.9 copy-start.26
  139.2 1.6 copy-start.27
  140.8 1.5 copy-start.25
  142.3 4.9 %copy-start.24 = (bf16[128,4,128]{2,1,0:T(4,128)(2,1)S(1)}, bf16[128,4,128]{2,1,0:T(4,128)(2,1)}, u32[]{:S(2)}) copy-start(bf16[128,4,128]{2,1,0:T(4,128)(2,1)} %slice.313) | copy-start | bytes 393220
  144.7 5.3 %copy-start.1 = (f32[512,1,512]{2,1,0:T(1,128)S(1)}, f32[512,1,512]{2,1,0:T(1,128)}, u32[]{:S(2)}) copy-start(f32[512,1,512]{2,1,0:T(1,128)} %get-tuple-element.103) | copy-start | bytes 3145732
  152.1 36.5 %all-to-all-start.3 = ((bf16[8,64,1,512]{3,1,2,0:T(8,128)(2,1)}), bf16[8,64,1,512]{3,1,2,0:T(8,128)(2,1)}, u32[]{:S(2)}, u32[]{:S(2)}) async-start(bf16[8,64,1,512]{3,1,2,0:T(8,128)(2,1)} %bitcast.254), calls=%async_computation.3 | async-start | bytes 1048576 | tf_op jit(solution)/shard_map/all_to_all | solution.py:165
  156.9 72.1 %reduce-scatter.2.cloned.1.call-start = ((), (), s32[]{:S(2)}) async-start(), calls=%async_computation.8 | async-start | bytes 1310720 | tf_op jit(solution)/shard_map/reduce_scatter | solution.py:150
  166.4 3.3 %copy-start.23 = (bf16[128,4,128]{2,1,0:T(4,128)(2,1)S(1)}, bf16[128,4,128]{2,1,0:T(4,128)(2,1)}, u32[]{:S(2)}) copy-start(bf16[128,4,128]{2,1,0:T(4,128)(2,1)} %slice.321) | copy-start | bytes 393220
  167.6 4.9 %copy-start.21 = (bf16[128,4,128]{2,1,0:T(4,128)(2,1)S(1)}, bf16[128,4,128]{2,1,0:T(4,128)(2,1)}, u32[]{:S(2)}) copy-start(bf16[128,4,128]{2,1,0:T(4,128)(2,1)} %slice.329) | copy-start | bytes 393220
  167.6 17.1 %collective-permute-start.11 = (bf16[2048,256]{1,0:T(8,128)(2,1)}, bf16[2048,256]{1,0:T(8,128)(2,1)}, u32[]{:S(2)}, u32[]{:S(2)}) collective-permute-start(bf16[2048,256]{1,0:T(8,128)(2,1)} %fusion.61), channel_id=1, source_target_pairs={{0,1},{1,0},{2,3},{3,2},{4,5},{5,4},{6,7},{7,6},{8,9},{9,8},{10,11... | collective-permute-start | bytes 3145736 | tf_op jit(solution)/shard_map/ppermute | solution.py:33
  180.7 3.9 %copy-start = (f32[2048,1,256]{2,0,1:T(8,128)S(1)}, f32[2048,1,256]{2,0,1:T(8,128)}, u32[]{:S(2)}) copy-start(f32[2048,1,256]{2,0,1:T(8,128)} %copy.245) | copy-start | bytes 6291460
  184.6 2.8 %copy-start.2 = (f32[512,1,512]{2,1,0:T(1,128)S(1)}, f32[512,1,512]{2,1,0:T(1,128)}, u32[]{:S(2)}) copy-start(f32[512,1,512]{2,1,0:T(1,128)} %get-tuple-element.105) | copy-start | bytes 3145732
  184.6 2.7 %collective-permute-start.9 = (bf16[512,512]{1,0:T(8,128)(2,1)}, bf16[512,512]{1,0:T(8,128)(2,1)}, u32[]{:S(2)}, u32[]{:S(2)}) collective-permute-start(bf16[512,512]{1,0:T(8,128)(2,1)} %bitcast.247), channel_id=1, source_target_pairs={{0,1},{1,0},{2,3},{3,2},{4,5},{5,4},{6,7},{7,6},{8,9},{9,8},{10,11... | collective-permute-start | bytes 1572872 | tf_op jit(solution)/shard_map/ppermute | solution.py:33
  208.6 18.8 %all-to-all-start.5 = ((bf16[8,64,1,512]{3,1,2,0:T(8,128)(2,1)}), bf16[8,64,1,512]{3,1,2,0:T(8,128)(2,1)S(1)}, u32[]{:S(2)}, u32[]{:S(2)}) async-start(bf16[8,64,1,512]{3,1,2,0:T(8,128)(2,1)} %bitcast.61), calls=%async_computation.5 | async-start | bytes 1048576 | tf_op jit(solution)/shard_map/all_to_all | solution.py:167
Sparse Core Ops, SparseCore 0:
  187.5 28.8 reduce-scatter.1
